TPU v7x, 512 devices: a whole 4x4x16 slice. The times are simulated.
512 devices in a mesh: rows: 512 (over y, z, x, core).
Axes of the slice: x: 4, y: 4, z: 16, core: 2. Of those that a mesh axis runs over, the one named last changes fastest.
Arguments:
- coupling: float32 [2048, 5, 128, 128], P('rows'), may hold values from -0.15 to 3.15, as said below
- columns: int32 [2048, 5], replicated, may hold values from 0 to 1023, as said below
- row_slots: int32 [1024], replicated, may hold values from 0 to 2047, as said below
Outputs:
- inverse_estimate: float32 [2048, 5, 128, 128], P('rows')
Inputs may be any that keep to these rules, and one draw needn't show every extreme that they name: `coupling`: in every slot the diagonal entries of tile 0 are at least 0.3. `columns`: for a slot that holds block row r, entry 0 is r and the other 4 entries are distinct block rows (r + d) mod 1024 with 1 <= |d| <= 3; entries of slots that hold no block row mean nothing. `row_slots`: device i owns slots i * 4 to (i + 1) * 4 - 1. Block rows are owned in order: device 0 holds the first ones, each device a contiguous run of rows in its first slots, at least 1 and at most 4 rows; some device holds 4.
All inputs are finite; a program needn't handle non-finite values.
Results may differ from a plain program's by a relative error of at most 0.0003.
Values sent between devices are 32-bit elements; how exact they have to be, the bound alone decides.
A program may use at most 64 MiB of HBM per device.

v0:
```python
import jax
import jax.numpy as jnp
from jax import lax
from jax.sharding import PartitionSpec as P

BAND = 3


precise = lax.Precision.HIGHEST


def from_behind(value, axis, steps):
    count = lax.axis_size(axis)
    pairs = [(source, (source + steps) % count) for source in range(count)]
    return lax.ppermute(value, axis, pairs)


def ownership(row_slots, slot_count, devices):
    owners = row_slots // slot_count
    listed = jnp.arange(devices, dtype=jnp.int32)
    counts = jnp.sum((owners[None, :] == listed[:, None]).astype(jnp.int32), axis=1)
    starts = jnp.cumsum(counts) - counts
    return (counts, starts)


def held_rows(counts, starts, device, first_slot, length):
    position = first_slot + jnp.arange(length, dtype=jnp.int32)
    return jnp.where(position < counts[device], starts[device] + position, -1)


def upper_start(counts, device, limit, slot_count):
    return jnp.clip(counts[device] - limit, 0, slot_count - limit)


def locate(wanted, row_ids):
    matches = wanted[..., None] == row_ids
    return jnp.argmax(matches, axis=-1)


def start_iterate(coupling, inverse, column_inverse):
    identity = jnp.eye(coupling.shape[-1], dtype=coupling.dtype)
    leading = (jnp.arange(coupling.shape[1]) == 0).astype(coupling.dtype)
    diagonal_part = 2.0 * leading[None, :, None, None] * (inverse[:, None, :, None] * identity)
    return diagonal_part - inverse[:, None, :, None] * coupling * column_inverse[:, :, None, :]


def pattern_product(left, row_pool, row_ids, pool_columns, own_columns):

    def per_slot(operands):
        blocks, row_columns = operands
        located = locate(row_columns, row_ids)
        fetched = jnp.take(row_pool, located, axis=0)
        their_columns = jnp.take(pool_columns, located, axis=0)
        selector = (their_columns[:, :, None] == row_columns[None, None, :]).astype(row_pool.dtype)
        chosen = jnp.einsum("kab,kaqr->kbqr", selector, fetched, precision=precise)
        return jnp.einsum("kpq,kbqr->bpr", blocks, chosen, precision=precise)

    return lax.map(per_slot, (left, own_columns))


def fetch_inverse(inverse, counts, starts, own_index, devices):
    slot_count = inverse.shape[0]
    pieces = [inverse]
    row_ids = [held_rows(counts, starts, own_index, 0, slot_count)]
    for offset in range(1, BAND + 1):
        for heading in (1, -1):
            pieces.append(from_behind(inverse, "rows", heading * offset))
            source = (own_index - heading * offset) % devices
            row_ids.append(held_rows(counts, starts, source, 0, slot_count))
    return (jnp.concatenate(pieces, 0), jnp.concatenate(row_ids, 0))


def fetch_tiles(shard, counts, starts, own_index, devices):
    slot_count = shard.shape[0]
    limits = [min(slot_count, BAND - offset + 1) for offset in range(1, BAND + 1)]
    pieces = [shard]
    row_ids = [held_rows(counts, starts, own_index, 0, slot_count)]
    for offset in range(1, BAND + 1):
        limit = limits[offset - 1]
        for heading in (1, -1):
            source = (own_index - heading * offset) % devices
            if heading > 0:
                first_slot = upper_start(counts, source, limit, slot_count)
                own_first = upper_start(counts, own_index, limit, slot_count)
            else:
                first_slot = 0
                own_first = 0
            outgoing = lax.dynamic_slice_in_dim(shard, own_first, limit, 0)
            pieces.append(from_behind(outgoing, "rows", heading * offset))
            row_ids.append(held_rows(counts, starts, source, first_slot, limit))
    return (jnp.concatenate(pieces, 0), jnp.concatenate(row_ids, 0))


def shards(coupling, columns, row_slots):
    slot_count = coupling.shape[0]
    devices = lax.axis_size("rows")
    own_index = lax.axis_index("rows")
    counts, starts = ownership(row_slots, slot_count, devices)
    own_columns = lax.dynamic_slice_in_dim(columns, own_index * slot_count, slot_count, 0)
    own_rows = held_rows(counts, starts, own_index, 0, slot_count)
    occupied = own_rows >= 0
    inverse = 1.0 / jnp.diagonal(coupling[:, 0], axis1=1, axis2=2)
    inverse_pool, inverse_ids = fetch_inverse(inverse, counts, starts, own_index, devices)
    column_inverse = jnp.take(inverse_pool, locate(own_columns, inverse_ids), axis=0)
    first_iterate = start_iterate(coupling, inverse, column_inverse)
    row_pool, row_ids = fetch_tiles(first_iterate, counts, starts, own_index, devices)
    pool_columns = jnp.take(columns, jnp.take(row_slots, jnp.maximum(row_ids, 0)), axis=0)
    product = pattern_product(coupling, row_pool, row_ids, pool_columns, own_columns)
    product_pool = fetch_tiles(product, counts, starts, own_index, devices)[0]
    second_iterate = 2.0 * first_iterate - pattern_product(
        first_iterate, product_pool, row_ids, pool_columns, own_columns
    )
    return jnp.where(occupied[:, None, None, None], second_iterate, 0.0)


def solution(mesh):
    return jax.shard_map(
        shards,
        mesh=mesh,
        in_specs=(P("rows", None, None, None), P(), P()),
        out_specs=P("rows", None, None, None),
        check_vma=False,
    )
```

profile of v0, /device:TPU:1, one launch (start us, length us, event | category | flops | bytes accessed | tf_op | source)
XLA Modules:
  0.0 284.7 jit_solution(6270061449167884925)
XLA Ops:
  1.0 4.7 %copy.99 = f32[4,1,128,128]{0,3,2,1:T(8,128)} copy(f32[4,1,128,128]{3,2,1,0:T(8,128)S(1)} %slice.12) | data formatting | bytes 524288
  7.5 4.6 %collective-permute-start = (f32[4,128]{0,1:T(8,128)S(1)}, f32[4,128]{0,1:T(8,128)S(1)}, u32[]{:S(2)}, u32[]{:S(2)}) collective-permute-start(f32[4,128]{0,1:T(8,128)S(1)} %divide_bitcast_fusion), channel_id=1, source_target_pairs={{0,1},{1,2},{2,3},{3,4},{4,5},{5,6},{6,7},{7,8},{8,9},{9,10},{10,1... | collective-permute-start | bytes 6152 | tf_op jit(solution)/shard_map/ppermute | solution.py:15
  12.1 6.2 %collective-permute-start.1 = (f32[4,128]{0,1:T(8,128)S(1)}, f32[4,128]{0,1:T(8,128)S(1)}, u32[]{:S(2)}, u32[]{:S(2)}) collective-permute-start(f32[4,128]{0,1:T(8,128)S(1)} %divide_bitcast_fusion), channel_id=1, source_target_pairs={{0,511},{1,0},{2,1},{3,2},{4,3},{5,4},{6,5},{7,6},{8,7},{9,8},{10,... | collective-permute-start | bytes 6152 | tf_op jit(solution)/shard_map/ppermute | solution.py:15
  20.2 10.4 %collective-permute-start.3 = (f32[4,128]{0,1:T(8,128)S(1)}, f32[4,128]{0,1:T(8,128)S(1)}, u32[]{:S(2)}, u32[]{:S(2)}) collective-permute-start(f32[4,128]{0,1:T(8,128)S(1)} %divide_bitcast_fusion), channel_id=1, source_target_pairs={{0,510},{1,511},{2,0},{3,1},{4,2},{5,3},{6,4},{7,5},{8,6},{9,7},{1... | collective-permute-start | bytes 6152 | tf_op jit(solution)/shard_map/ppermute | solution.py:15
  58.9 9.1 %collective-permute-start.5 = (f32[4,128]{0,1:T(8,128)S(1)}, f32[4,128]{0,1:T(8,128)S(1)}, u32[]{:S(2)}, u32[]{:S(2)}) collective-permute-start(f32[4,128]{0,1:T(8,128)S(1)} %divide_bitcast_fusion), channel_id=1, source_target_pairs={{0,509},{1,510},{2,511},{3,0},{4,1},{5,2},{6,3},{7,4},{8,5},{9,6},... | collective-permute-start | bytes 6152 | tf_op jit(solution)/shard_map/ppermute | solution.py:15
  78.5 7.7 %collective-permute-start.7 = (f32[3,5,128,128]{3,2,1,0:T(8,128)}, f32[3,5,128,128]{3,2,1,0:T(8,128)}, u32[]{:S(2)}, u32[]{:S(2)}) collective-permute-start(f32[3,5,128,128]{3,2,1,0:T(8,128)} %get-tuple-element.185), channel_id=1, source_target_pairs={{0,511},{1,0},{2,1},{3,2},{4,3},{5,4},{6,5},{7,6},{8,7},{9,8},{10,... | collective-permute-start | bytes 2949128 | tf_op jit(solution)/shard_map/ppermute | solution.py:15
  91.1 8.8 %collective-permute-start.9 = (f32[2,5,128,128]{3,2,1,0:T(8,128)}, f32[2,5,128,128]{3,2,1,0:T(8,128)S(1)}, u32[]{:S(2)}, u32[]{:S(2)}) collective-permute-start(f32[2,5,128,128]{3,2,1,0:T(8,128)} %get-tuple-element.183), channel_id=1, source_target_pairs={{0,510},{1,511},{2,0},{3,1},{4,2},{5,3},{6,4},{7,5},{8,6},{9,7},{1... | collective-permute-start | bytes 1966088 | tf_op jit(solution)/shard_map/ppermute | solution.py:15
  102.7 9.2 %collective-permute-start.11 = (f32[1,5,128,128]{3,2,1,0:T(8,128)S(1)}, f32[1,5,128,128]{3,2,1,0:T(8,128)S(1)}, u32[]{:S(2)}, u32[]{:S(2)}) collective-permute-start(f32[1,5,128,128]{3,2,1,0:T(8,128)S(1)} %get-tuple-element.181), channel_id=1, source_target_pairs={{0,509},{1,510},{2,511},{3,0},{4,1},{5,2},{6,3},{7,4},{8,5},{9,6},... | collective-permute-start | bytes 983048 | tf_op jit(solution)/shard_map/ppermute | solution.py:15
  120.3 8.1 %collective-permute-done.10 = f32[1,5,128,128]{3,2,1,0:T(8,128)S(1)} collective-permute-done((f32[1,5,128,128]{3,2,1,0:T(8,128)S(1)}, f32[1,5,128,128]{3,2,1,0:T(8,128)S(1)}, u32[]{:S(2)}, u32[]{:S(2)}) %collective-permute-start.10) | collective-permute-done | bytes 327712 | tf_op jit(solution)/shard_map/ppermute | solution.py:15
  131.1 47.4 %while.20 = (s32[]{:T(128)}, f32[4,5,128,128]{3,2,1,0:T(8,128)}, s32[4,5]{1,0:T(4,128)S(1)}, s32[16]{0:T(128)S(1)}, s32[16,5]{1,0:T(8,128)S(1)}, /*index=5*/f32[...) while((s32[]{:T(128)}, f32[4,5,128,128]{3,2,1,0:T(8,128)}, ...), condition=%wide.region_6.9_spmd, body=%wide.region_4.8_spmd.sunk | while | flops 654132992 | bytes 18683808 | solution.py:58
  138.1 3.9 %fusion.66 = f32[1,5,128,128]{2,3,1,0:T(8,128)S(1)} fusion(f32[5,5,128,128]{3,1,2,0:T(8,128)S(1)} %fusion.65, f32[4,5,128,128]{3,2,1,0:T(8,128)} %get-tuple-element.356, s32[]{:T(128)} %get-tuple-element.306), kind=kOutput, calls=%fused_computation.12.clone.1 | convolution fusion | flops 629145600 | bytes 2294272 | tf_op jit(solution)/shard_map/while/body/eval_jaxpr/kpq,kbqr->bpr/dot_general | solution.py:56
  150.0 3.9 %fusion.66 = f32[1,5,128,128]{2,3,1,0:T(8,128)S(1)} fusion(f32[5,5,128,128]{3,1,2,0:T(8,128)S(1)} %fusion.65, f32[4,5,128,128]{3,2,1,0:T(8,128)} %get-tuple-element.356, s32[]{:T(128)} %get-tuple-element.306), kind=kOutput, calls=%fused_computation.12.clone.1 | convolution fusion | flops 629145600 | bytes 2294272 | tf_op jit(solution)/shard_map/while/body/eval_jaxpr/kpq,kbqr->bpr/dot_general | solution.py:56
  161.8 3.9 %fusion.66 = f32[1,5,128,128]{2,3,1,0:T(8,128)S(1)} fusion(f32[5,5,128,128]{3,1,2,0:T(8,128)S(1)} %fusion.65, f32[4,5,128,128]{3,2,1,0:T(8,128)} %get-tuple-element.356, s32[]{:T(128)} %get-tuple-element.306), kind=kOutput, calls=%fused_computation.12.clone.1 | convolution fusion | flops 629145600 | bytes 2294272 | tf_op jit(solution)/shard_map/while/body/eval_jaxpr/kpq,kbqr->bpr/dot_general | solution.py:56
  173.7 3.9 %fusion.66 = f32[1,5,128,128]{2,3,1,0:T(8,128)S(1)} fusion(f32[5,5,128,128]{3,1,2,0:T(8,128)S(1)} %fusion.65, f32[4,5,128,128]{3,2,1,0:T(8,128)} %get-tuple-element.356, s32[]{:T(128)} %get-tuple-element.306), kind=kOutput, calls=%fused_computation.12.clone.1 | convolution fusion | flops 629145600 | bytes 2294272 | tf_op jit(solution)/shard_map/while/body/eval_jaxpr/kpq,kbqr->bpr/dot_general | solution.py:56
  182.3 6.1 %collective-permute-start.13 = (f32[3,5,128,128]{3,2,1,0:T(8,128)S(1)}, f32[3,5,128,128]{3,2,1,0:T(8,128)S(1)}, u32[]{:S(2)}, u32[]{:S(2)}) collective-permute-start(f32[3,5,128,128]{3,2,1,0:T(8,128)S(1)} %get-tuple-element.179), channel_id=1, source_target_pairs={{0,511},{1,0},{2,1},{3,2},{4,3},{5,4},{6,5},{7,6},{8,7},{9,8},{10,... | collective-permute-start | bytes 2949128 | tf_op jit(solution)/shard_map/ppermute | solution.py:15
  190.5 8.8 %collective-permute-start.15 = (f32[2,5,128,128]{3,2,1,0:T(8,128)S(1)}, f32[2,5,128,128]{3,2,1,0:T(8,128)S(1)}, u32[]{:S(2)}, u32[]{:S(2)}) collective-permute-start(f32[2,5,128,128]{3,2,1,0:T(8,128)S(1)} %get-tuple-element.177), channel_id=1, source_target_pairs={{0,510},{1,511},{2,0},{3,1},{4,2},{5,3},{6,4},{7,5},{8,6},{9,7},{1... | collective-permute-start | bytes 1966088 | tf_op jit(solution)/shard_map/ppermute | solution.py:15
  201.4 14.5 %collective-permute-start.17 = (f32[1,5,128,128]{3,2,1,0:T(8,128)S(1)}, f32[1,5,128,128]{3,2,1,0:T(8,128)S(1)}, u32[]{:S(2)}, u32[]{:S(2)}) collective-permute-start(f32[1,5,128,128]{3,2,1,0:T(8,128)S(1)} %get-tuple-element.175), channel_id=1, source_target_pairs={{0,509},{1,510},{2,511},{3,0},{4,1},{5,2},{6,3},{7,4},{8,5},{9,6},... | collective-permute-start | bytes 983048 | tf_op jit(solution)/shard_map/ppermute | solution.py:15
  216.1 9.4 %collective-permute-done.14 = f32[2,5,128,128]{3,2,1,0:T(8,128)S(1)} collective-permute-done((f32[2,5,128,128]{3,2,1,0:T(8,128)S(1)}, f32[2,5,128,128]{3,2,1,0:T(8,128)S(1)}, u32[]{:S(2)}, u32[]{:S(2)}) %collective-permute-start.14) | collective-permute-done | bytes 655392 | tf_op jit(solution)/shard_map/ppermute | solution.py:15
  225.6 6.3 %collective-permute-done.16 = f32[1,5,128,128]{3,2,1,0:T(8,128)S(1)} collective-permute-done((f32[1,5,128,128]{3,2,1,0:T(8,128)S(1)}, f32[1,5,128,128]{3,2,1,0:T(8,128)S(1)}, u32[]{:S(2)}, u32[]{:S(2)}) %collective-permute-start.16) | collective-permute-done | bytes 327712 | tf_op jit(solution)/shard_map/ppermute | solution.py:15
  234.7 47.0 %while.21 = (s32[]{:T(128)}, f32[4,5,128,128]{3,2,1,0:T(8,128)}, s32[4,5]{1,0:T(4,128)S(1)}, s32[16]{0:T(128)S(1)}, s32[16,5]{1,0:T(8,128)S(1)}, /*index=5*/f32[...) while((s32[]{:T(128)}, f32[4,5,128,128]{3,2,1,0:T(8,128)}, s32[4,5]{1,0:T(4,128)S(1)}, ...), condition=%wide.region_9.12_spmd, body=%wide.region_7.11_spmd.sunk | while | flops 654132992 | bytes 13440893 | solution.py:58
  241.7 3.8 %fusion.73 = f32[1,5,128,128]{2,3,1,0:T(8,128)S(1)} fusion(f32[5,5,128,128]{3,1,2,0:T(8,128)S(1)} %fusion.72, f32[4,5,128,128]{3,2,1,0:T(8,128)} %get-tuple-element.344, s32[]{:T(128)} %get-tuple-element.330), kind=kOutput, calls=%fused_computation.33.clone.1 | convolution fusion | flops 629145600 | bytes 2294272 | tf_op jit(solution)/shard_map/while/body/eval_jaxpr/kpq,kbqr->bpr/dot_general | solution.py:56
  253.4 3.8 %fusion.73 = f32[1,5,128,128]{2,3,1,0:T(8,128)S(1)} fusion(f32[5,5,128,128]{3,1,2,0:T(8,128)S(1)} %fusion.72, f32[4,5,128,128]{3,2,1,0:T(8,128)} %get-tuple-element.344, s32[]{:T(128)} %get-tuple-element.330), kind=kOutput, calls=%fused_computation.33.clone.1 | convolution fusion | flops 629145600 | bytes 2294272 | tf_op jit(solution)/shard_map/while/body/eval_jaxpr/kpq,kbqr->bpr/dot_general | solution.py:56
  265.2 3.8 %fusion.73 = f32[1,5,128,128]{2,3,1,0:T(8,128)S(1)} fusion(f32[5,5,128,128]{3,1,2,0:T(8,128)S(1)} %fusion.72, f32[4,5,128,128]{3,2,1,0:T(8,128)} %get-tuple-element.344, s32[]{:T(128)} %get-tuple-element.330), kind=kOutput, calls=%fused_computation.33.clone.1 | convolution fusion | flops 629145600 | bytes 2294272 | tf_op jit(solution)/shard_map/while/body/eval_jaxpr/kpq,kbqr->bpr/dot_general | solution.py:56
  276.9 3.8 %fusion.73 = f32[1,5,128,128]{2,3,1,0:T(8,128)S(1)} fusion(f32[5,5,128,128]{3,1,2,0:T(8,128)S(1)} %fusion.72, f32[4,5,128,128]{3,2,1,0:T(8,128)} %get-tuple-element.344, s32[]{:T(128)} %get-tuple-element.330), kind=kOutput, calls=%fused_computation.33.clone.1 | convolution fusion | flops 629145600 | bytes 2294272 | tf_op jit(solution)/shard_map/while/body/eval_jaxpr/kpq,kbqr->bpr/dot_general | solution.py:56
  (226 shorter events, 132.8 us)
Async XLA Ops:
  1.0 31.8 %copy-start = (s32[1024]{0:T(1024)S(1)}, s32[1024]{0:T(1024)}, u32[]{:S(2)}) copy-start(s32[1024]{0:T(1024)} %param.13) | copy-start | bytes 12292
  1.0 32.7 %copy-start.7 = (s32[2048,5]{0,1:T(8,128)S(1)}, s32[2048,5]{0,1:T(8,128)}, u32[]{:S(2)}) copy-start(s32[2048,5]{0,1:T(8,128)} %param.12) | copy-start | bytes 122884
  7.5 64.5 %copy-start.4 = (f32[4,5,128,128]{3,2,1,0:T(8,128)S(1)}, f32[4,5,128,128]{3,2,1,0:T(8,128)}, u32[]{:S(2)}) copy-start(f32[4,5,128,128]{3,2,1,0:T(8,128)} %param.11) | copy-start | bytes 3932164
  7.5 51.4 %collective-permute-start = (f32[4,128]{0,1:T(8,128)S(1)}, f32[4,128]{0,1:T(8,128)S(1)}, u32[]{:S(2)}, u32[]{:S(2)}) collective-permute-start(f32[4,128]{0,1:T(8,128)S(1)} %divide_bitcast_fusion), channel_id=1, source_target_pairs={{0,1},{1,2},{2,3},{3,4},{4,5},{5,6},{6,7},{7,8},{8,9},{9,10},{10,1... | collective-permute-start | bytes 6152 | tf_op jit(solution)/shard_map/ppermute | solution.py:15
  12.1 58.7 %collective-permute-start.1 = (f32[4,128]{0,1:T(8,128)S(1)}, f32[4,128]{0,1:T(8,128)S(1)}, u32[]{:S(2)}, u32[]{:S(2)}) collective-permute-start(f32[4,128]{0,1:T(8,128)S(1)} %divide_bitcast_fusion), channel_id=1, source_target_pairs={{0,511},{1,0},{2,1},{3,2},{4,3},{5,4},{6,5},{7,6},{8,7},{9,8},{10,... | collective-permute-start | bytes 6152 | tf_op jit(solution)/shard_map/ppermute | solution.py:15
  18.3 52.6 %collective-permute-start.2 = (f32[4,128]{0,1:T(8,128)S(1)}, f32[4,128]{0,1:T(8,128)S(1)}, u32[]{:S(2)}, u32[]{:S(2)}) collective-permute-start(f32[4,128]{0,1:T(8,128)S(1)} %divide_bitcast_fusion), channel_id=1, source_target_pairs={{0,2},{1,3},{2,4},{3,5},{4,6},{5,7},{6,8},{7,9},{8,10},{9,11},{10,... | collective-permute-start | bytes 6152 | tf_op jit(solution)/shard_map/ppermute | solution.py:15
  20.2 50.8 %collective-permute-start.3 = (f32[4,128]{0,1:T(8,128)S(1)}, f32[4,128]{0,1:T(8,128)S(1)}, u32[]{:S(2)}, u32[]{:S(2)}) collective-permute-start(f32[4,128]{0,1:T(8,128)S(1)} %divide_bitcast_fusion), channel_id=1, source_target_pairs={{0,510},{1,511},{2,0},{3,1},{4,2},{5,3},{6,4},{7,5},{8,6},{9,7},{1... | collective-permute-start | bytes 6152 | tf_op jit(solution)/shard_map/ppermute | solution.py:15
  30.7 40.4 %collective-permute-start.4 = (f32[4,128]{0,1:T(8,128)S(1)}, f32[4,128]{0,1:T(8,128)S(1)}, u32[]{:S(2)}, u32[]{:S(2)}) collective-permute-start(f32[4,128]{0,1:T(8,128)S(1)} %divide_bitcast_fusion), channel_id=1, source_target_pairs={{0,3},{1,4},{2,5},{3,6},{4,7},{5,8},{6,9},{7,10},{8,11},{9,12},{10... | collective-permute-start | bytes 6152 | tf_op jit(solution)/shard_map/ppermute | solution.py:15
  34.1 37.1 %copy-start.6 = (s32[2048,5]{1,0:T(8,128)}, s32[2048,5]{1,0:T(8,128)S(1)}, u32[]{:S(2)}) copy-start(s32[2048,5]{1,0:T(8,128)S(1)} %copy.69) | copy-start | bytes 122884
  58.9 12.2 %collective-permute-start.5 = (f32[4,128]{0,1:T(8,128)S(1)}, f32[4,128]{0,1:T(8,128)S(1)}, u32[]{:S(2)}, u32[]{:S(2)}) collective-permute-start(f32[4,128]{0,1:T(8,128)S(1)} %divide_bitcast_fusion), channel_id=1, source_target_pairs={{0,509},{1,510},{2,511},{3,0},{4,1},{5,2},{6,3},{7,4},{8,5},{9,6},... | collective-permute-start | bytes 6152 | tf_op jit(solution)/shard_map/ppermute | solution.py:15
  73.4 27.2 %copy-start.1 = (f32[4,5,128,128]{3,2,1,0:T(8,128)}, f32[4,5,128,128]{3,2,1,0:T(8,128)S(1)}, u32[]{:S(2)}) copy-start(f32[4,5,128,128]{3,2,1,0:T(8,128)S(1)} %get-tuple-element.328) | copy-start | bytes 3932164
  75.0 27.7 %collective-permute-start.6 = (f32[3,5,128,128]{3,2,1,0:T(8,128)}, f32[3,5,128,128]{3,2,1,0:T(8,128)}, u32[]{:S(2)}, u32[]{:S(2)}) collective-permute-start(f32[3,5,128,128]{3,2,1,0:T(8,128)} %get-tuple-element.186), channel_id=1, source_target_pairs={{0,1},{1,2},{2,3},{3,4},{4,5},{5,6},{6,7},{7,8},{8,9},{9,10},{10,1... | collective-permute-start | bytes 2949128 | tf_op jit(solution)/shard_map/ppermute | solution.py:15
  78.5 35.7 %collective-permute-start.7 = (f32[3,5,128,128]{3,2,1,0:T(8,128)}, f32[3,5,128,128]{3,2,1,0:T(8,128)}, u32[]{:S(2)}, u32[]{:S(2)}) collective-permute-start(f32[3,5,128,128]{3,2,1,0:T(8,128)} %get-tuple-element.185), channel_id=1, source_target_pairs={{0,511},{1,0},{2,1},{3,2},{4,3},{5,4},{6,5},{7,6},{8,7},{9,8},{10,... | collective-permute-start | bytes 2949128 | tf_op jit(solution)/shard_map/ppermute | solution.py:15
  89.2 27.4 %collective-permute-start.8 = (f32[2,5,128,128]{3,2,1,0:T(8,128)}, f32[2,5,128,128]{3,2,1,0:T(8,128)}, u32[]{:S(2)}, u32[]{:S(2)}) collective-permute-start(f32[2,5,128,128]{3,2,1,0:T(8,128)} %get-tuple-element.184), channel_id=1, source_target_pairs={{0,2},{1,3},{2,4},{3,5},{4,6},{5,7},{6,8},{7,9},{8,10},{9,11},{10,... | collective-permute-start | bytes 1966088 | tf_op jit(solution)/shard_map/ppermute | solution.py:15
  91.1 28.3 %collective-permute-start.9 = (f32[2,5,128,128]{3,2,1,0:T(8,128)}, f32[2,5,128,128]{3,2,1,0:T(8,128)S(1)}, u32[]{:S(2)}, u32[]{:S(2)}) collective-permute-start(f32[2,5,128,128]{3,2,1,0:T(8,128)} %get-tuple-element.183), channel_id=1, source_target_pairs={{0,510},{1,511},{2,0},{3,1},{4,2},{5,3},{6,4},{7,5},{8,6},{9,7},{1... | collective-permute-start | bytes 1966088 | tf_op jit(solution)/shard_map/ppermute | solution.py:15
  100.7 27.6 %collective-permute-start.10 = (f32[1,5,128,128]{3,2,1,0:T(8,128)S(1)}, f32[1,5,128,128]{3,2,1,0:T(8,128)S(1)}, u32[]{:S(2)}, u32[]{:S(2)}) collective-permute-start(f32[1,5,128,128]{3,2,1,0:T(8,128)S(1)} %get-tuple-element.182), channel_id=1, source_target_pairs={{0,3},{1,4},{2,5},{3,6},{4,7},{5,8},{6,9},{7,10},{8,11},{9,12},{10... | collective-permute-start | bytes 983048 | tf_op jit(solution)/shard_map/ppermute | solution.py:15
  102.7 26.4 %collective-permute-start.11 = (f32[1,5,128,128]{3,2,1,0:T(8,128)S(1)}, f32[1,5,128,128]{3,2,1,0:T(8,128)S(1)}, u32[]{:S(2)}, u32[]{:S(2)}) collective-permute-start(f32[1,5,128,128]{3,2,1,0:T(8,128)S(1)} %get-tuple-element.181), channel_id=1, source_target_pairs={{0,509},{1,510},{2,511},{3,0},{4,1},{5,2},{6,3},{7,4},{8,5},{9,6},... | collective-permute-start | bytes 983048 | tf_op jit(solution)/shard_map/ppermute | solution.py:15
  178.5 9.9 %copy-start.2 = (f32[4,5,128,128]{3,2,1,0:T(8,128)S(1)}, f32[4,5,128,128]{3,2,1,0:T(8,128)}, u32[]{:S(2)}) copy-start(f32[4,5,128,128]{3,2,1,0:T(8,128)} %get-tuple-element.349) | copy-start | bytes 3932164
  180.4 21.0 %collective-permute-start.12 = (f32[3,5,128,128]{3,2,1,0:T(8,128)S(1)}, f32[3,5,128,128]{3,2,1,0:T(8,128)S(1)}, u32[]{:S(2)}, u32[]{:S(2)}) collective-permute-start(f32[3,5,128,128]{3,2,1,0:T(8,128)S(1)} %get-tuple-element.180), channel_id=1, source_target_pairs={{0,1},{1,2},{2,3},{3,4},{4,5},{5,6},{6,7},{7,8},{8,9},{9,10},{10,1... | collective-permute-start | bytes 2949128 | tf_op jit(solution)/shard_map/ppermute | solution.py:15
  182.3 33.7 %collective-permute-start.13 = (f32[3,5,128,128]{3,2,1,0:T(8,128)S(1)}, f32[3,5,128,128]{3,2,1,0:T(8,128)S(1)}, u32[]{:S(2)}, u32[]{:S(2)}) collective-permute-start(f32[3,5,128,128]{3,2,1,0:T(8,128)S(1)} %get-tuple-element.179), channel_id=1, source_target_pairs={{0,511},{1,0},{2,1},{3,2},{4,3},{5,4},{6,5},{7,6},{8,7},{9,8},{10,... | collective-permute-start | bytes 2949128 | tf_op jit(solution)/shard_map/ppermute | solution.py:15
  188.6 37.0 %collective-permute-start.14 = (f32[2,5,128,128]{3,2,1,0:T(8,128)S(1)}, f32[2,5,128,128]{3,2,1,0:T(8,128)S(1)}, u32[]{:S(2)}, u32[]{:S(2)}) collective-permute-start(f32[2,5,128,128]{3,2,1,0:T(8,128)S(1)} %get-tuple-element.178), channel_id=1, source_target_pairs={{0,2},{1,3},{2,4},{3,5},{4,6},{5,7},{6,8},{7,9},{8,10},{9,11},{10,... | collective-permute-start | bytes 1966088 | tf_op jit(solution)/shard_map/ppermute | solution.py:15
  190.5 35.1 %collective-permute-start.15 = (f32[2,5,128,128]{3,2,1,0:T(8,128)S(1)}, f32[2,5,128,128]{3,2,1,0:T(8,128)S(1)}, u32[]{:S(2)}, u32[]{:S(2)}) collective-permute-start(f32[2,5,128,128]{3,2,1,0:T(8,128)S(1)} %get-tuple-element.177), channel_id=1, source_target_pairs={{0,510},{1,511},{2,0},{3,1},{4,2},{5,3},{6,4},{7,5},{8,6},{9,7},{1... | collective-permute-start | bytes 1966088 | tf_op jit(solution)/shard_map/ppermute | solution.py:15
  199.3 32.6 %collective-permute-start.16 = (f32[1,5,128,128]{3,2,1,0:T(8,128)S(1)}, f32[1,5,128,128]{3,2,1,0:T(8,128)S(1)}, u32[]{:S(2)}, u32[]{:S(2)}) collective-permute-start(f32[1,5,128,128]{3,2,1,0:T(8,128)S(1)} %get-tuple-element.176), channel_id=1, source_target_pairs={{0,3},{1,4},{2,5},{3,6},{4,7},{5,8},{6,9},{7,10},{8,11},{9,12},{10... | collective-permute-start | bytes 983048 | tf_op jit(solution)/shard_map/ppermute | solution.py:15
  201.4 30.5 %collective-permute-start.17 = (f32[1,5,128,128]{3,2,1,0:T(8,128)S(1)}, f32[1,5,128,128]{3,2,1,0:T(8,128)S(1)}, u32[]{:S(2)}, u32[]{:S(2)}) collective-permute-start(f32[1,5,128,128]{3,2,1,0:T(8,128)S(1)} %get-tuple-element.175), channel_id=1, source_target_pairs={{0,509},{1,510},{2,511},{3,0},{4,1},{5,2},{6,3},{7,4},{8,5},{9,6},... | collective-permute-start | bytes 983048 | tf_op jit(solution)/shard_map/ppermute | solution.py:15
  (5 other events, 22.0 us)
where the time goes:
time: 286 us; the launch traced here: 285 us
  starting transfers between devices  102 us (36%)
  local copies, waits for them, and re-layouts  68.1 us (24%)
  matrix products  48.4 us (17%)
  other arithmetic  33.7 us (12%)
  waiting for transfers between devices  24.8 us (9%)
  between operations  6.9 us (2%)
    ppermute x18, starting transfers between devices, from_behind(): return lax.ppermute(value, axis, pairs)  102 us
    dot_general x8, matrix products, per_slot(): return jnp.einsum('kpq,kbqr->bpr', blocks, chosen, precision=precise)  30.7 us
    gather x8, local copies, waits for them, and re-layouts, per_slot(): fetched = jnp.take(row_pool, located, axis=0)  25.1 us
    ppermute x18, waiting for transfers between devices, from_behind(): return lax.ppermute(value, axis, pairs)  24.8 us
    dot_general x8, matrix products, per_slot(): chosen = jnp.einsum('kab,kaqr->kbqr', selector, fetched, precision=precise)  17.7 us
    unnamed x27, local copies, waits for them, and re-layouts  14.9 us
    select_n x10, other arithmetic, held_rows(): return jnp.where(position < counts[device], starts[device] + position, -1)  12.4 us
    dynamic_update_slice x16, local copies, waits for them, and re-layouts, pattern_product(): return lax.map(per_slot, (left, own_columns))  7.33 us
  transfers between devices with their start and end apart: 18, of which 5 were waited for; matrix products, arithmetic and copies ran while one was open for 12% of the time, Pallas kernels for 0%

commit v1 on v0

v1 whole, which is shorter than its diff:
```python
import functools

import jax
import jax.numpy as jnp
from jax import lax
from jax.experimental import pallas as pl
from jax.experimental.pallas import tpu as pltpu
from jax.sharding import PartitionSpec as P

TILE = 128
TILES = 5
SLOT = 4
BAND = 3
AXIS = "rows"
MESH = pl.DeviceIdType.MESH

WIDTHS = (5, 5, 5, 3, 2, 1)

WHOLE = 10 * TILES
PARTS = WIDTHS[3:]
ZERO = WHOLE + 2 * sum(PARTS)
PLACES = 16
SPAN = 2 * BAND + 1
NAMES = TILES * TILES


def first_row(slots_ref, bound):
    found = jnp.int32(0)
    step = slots_ref.shape[0] // 2
    while step:
        below = slots_ref[found + step - 1] < bound
        found = found + jnp.where(below, step, 0)
        step //= 2
    return found


def ownership(slots_ref, me):
    rows = slots_ref.shape[0]
    start = first_row(slots_ref, me * SLOT)
    count = jnp.int32(1)
    for k in range(1, SLOT):
        at = start + k
        inside = slots_ref[jnp.minimum(at, rows - 1)] < (me + 1) * SLOT
        count = count + jnp.where(jnp.logical_and(at < rows, inside), 1, 0)
    return start, count


def wrapped(value, rows):
    return lax.rem(value + rows, rows)


def signed(value, rows):
    half = rows // 2
    return lax.rem(value + rows + half, rows) - half


def inverse_column(tile, eye):
    return 1.0 / jnp.sum(jnp.where(eye, tile, 0.0), axis=1, keepdims=True)


def inverse_row(tile, eye):
    return 1.0 / jnp.sum(jnp.where(eye, tile, 0.0), axis=0, keepdims=True)


def split(value):
    high = value.astype(jnp.bfloat16)
    low = (value - high.astype(jnp.float32)).astype(jnp.bfloat16)
    return high, low


def dot(left, right):
    return jnp.dot(left, right, preferred_element_type=jnp.float32)


def multiply(left_high, left_low, base, pool_high, pool_low, names_ref, named):
    def block(pool, us, ts):
        return jnp.concatenate(
            [
                jnp.concatenate([pool[names_ref[named + u * TILES + t]] for t in ts], axis=1)
                for u in us
            ],
            axis=0,
        )

    def left(us):
        high = jnp.concatenate([left_high[base + u] for u in us], axis=1)
        low = jnp.concatenate([left_low[base + u] for u in us], axis=1)
        return high, jnp.concatenate([high, low], axis=0)

    pairs = ((0, 1), (2, 3))
    out = []
    for ts in pairs:
        total = None
        rest = None
        for us in pairs:
            high, both = left(us)
            part = dot(both, block(pool_high, us, ts))
            more = dot(high, block(pool_low, us, ts))
            total = part if total is None else total + part
            rest = more if rest is None else rest + more
        high = left_high[base + 4]
        low = left_low[base + 4]
        last = jnp.concatenate(
            [
                jnp.concatenate([high, high], axis=1),
                jnp.concatenate([low, jnp.zeros_like(low)], axis=1),
            ],
            axis=0,
        )
        right = jnp.concatenate([block(pool_high, (4,), ts), block(pool_low, (4,), ts)], axis=0)
        total = total + dot(last, right)
        value = total[:TILE] + total[TILE:] + rest
        out.append(value[:, :TILE])
        out.append(value[:, TILE:])
    total = None
    for us in pairs + ((4,),):
        right = jnp.concatenate([block(pool_high, us, (4,)), block(pool_low, us, (4,))], axis=1)
        part = dot(left(us)[1], right)
        total = part if total is None else total + part
    out.append(total[:TILE, :TILE] + (total[TILE:, :TILE] + total[:TILE, TILE:]))
    return out


def kernel(devices, own_hbm, columns_hbm, slots_ref, out_ref, own_ref, columns_ref, *refs):
    arriving = (refs[0:6], refs[6:12])
    leaving = (refs[12:18], refs[18:24])
    e_high, e_low, f_high, f_low, inverses, tiles, offsets, names = refs[24:32]
    send_sem, recv_sem, own_sem, columns_sem = refs[32:]
    rows = slots_ref.shape[0]
    me = lax.axis_index(AXIS)
    right, left = lax.rem(me + 1, devices), lax.rem(me + devices - 1, devices)
    odd = lax.rem(me, 2) == 1
    outward = jnp.where(odd, right, left)
    partner = jnp.where(odd, left, right)
    heading = (jnp.where(odd, 1, -1), jnp.where(odd, -1, 1))

    barrier = pltpu.get_barrier_semaphore()
    for other in (left, right):
        pl.semaphore_signal(barrier, inc=1, device_id=(other,), device_id_type=MESH)
    fetch = pltpu.make_async_copy(own_hbm, own_ref, own_sem)
    fetch.start()
    fetch_columns = pltpu.make_async_copy(columns_hbm, columns_ref, columns_sem)
    fetch_columns.start()

    start, count = ownership(slots_ref, me)
    shape = (TILE, TILE)
    eye = lax.broadcasted_iota(jnp.int32, shape, 0) == lax.broadcasted_iota(jnp.int32, shape, 1)

    fetch.wait()
    pl.semaphore_wait(barrier, 2)

    def copy(side, k):
        return pltpu.make_async_remote_copy(
            src_ref=leaving[side][k],
            dst_ref=arriving[1 - side][k],
            send_sem=send_sem.at[side, k],
            recv_sem=recv_sem.at[1 - side, k],
            device_id=((outward, partner)[side],),
            device_id_type=MESH,
        )

    def await_row(side, k):
        copy(1 - side, k).wait_recv()

    def own_slot(side, k):
        return jnp.where(heading[side] > 0, jnp.maximum(count - 1 - k, 0), k)

    def fill_whole(side, k):
        received = arriving[side]
        target = leaving[side][k]
        for t in range(TILES):
            value = own_ref[own_slot(side, k), t]
            for held in range(1, k + 1):
                value = jnp.where(count == held, received[k - held][t], value)
            target[t] = value

    def tile_at_offset(row, offset):
        slot = slots_ref[row]
        target = wrapped(row + offset, rows)
        found = jnp.int32(0)
        for v in range(1, TILES):
            found = jnp.where(columns_ref[v, slot] == target, v, found)
        return found

    def fill_part(side, k):
        received = arriving[side]
        target = leaving[side][k]
        row = wrapped(jnp.where(heading[side] > 0, start + count - 1 - k, start + k), rows)
        whole = [(held, k - held) for held in range(1, SLOT + 1) if 0 <= k - held <= 2]
        diagonal = own_ref[own_slot(side, k), 0] if k == 3 else None
        for held, position in whole:
            tile = received[position][0]
            diagonal = tile if diagonal is None else jnp.where(count == held, tile, diagonal)
        scale = inverse_column(diagonal, eye)
        for place in range(WIDTHS[k]):
            offset = heading[side] * (BAND - WIDTHS[k] + 1 + place)
            index = tile_at_offset(row, offset)
            value = own_ref[own_slot(side, k), index] if k == 3 else None
            for held, position in whole:
                tile = received[position][index]
                value = tile if value is None else jnp.where(count == held, tile, value)
            value = jnp.where(index > 0, -(scale * value), 0.0)
            for held in range(1, SLOT + 1):
                position = k - held
                if position > 2:
                    ready = received[position][WIDTHS[position] - WIDTHS[k] + place]
                    value = jnp.where(count == held, ready, value)
            target[place] = value

    def forward(side, k):
        if k < 3:
            fill_whole(side, k)
        else:
            fill_part(side, k)
        copy(side, k).start()

    def distance(side, k):
        return jnp.where(heading[side] > 0, -1 - k, count + k)

    def place_of(d):
        below = jnp.where(odd, 6 + d, 9 - d)
        above = jnp.where(odd, 10 + d - count, 5 - d + count)
        return jnp.where(d < 0, below, jnp.where(d < count, 6 + d, above))

    def row_place(f):
        return 6 + f if f < 4 else (9 - f if f < 7 else 3 + f)

    def row_distance(f):
        return jnp.int32(f) if f < 4 else distance((f - 4) // 3, (f - 4) % 3)

    def convert_whole(f):
        source = own_ref.at[f] if f < 4 else arriving[(f - 4) // 3][(f - 4) % 3]
        diagonal = source[0]
        scale = inverse_column(diagonal, eye)
        inverses[row_place(f)] = jnp.broadcast_to(inverse_row(diagonal, eye), (8, TILE))
        for v in range(TILES):
            value = -(scale * source[v])
            if v == 0:
                value = jnp.where(eye, 1.0, 0.0) + value
            e_high[f * TILES + v], e_low[f * TILES + v] = split(value)

    def part_index(side, k):
        return WHOLE + side * sum(PARTS) + sum(PARTS[: k - 3])

    def convert_part(side, k):
        at = part_index(side, k)
        for n in range(WIDTHS[k]):
            e_high[at + n], e_low[at + n] = split(arriving[side][k][n])

    forward(0, 0)
    forward(1, 0)

    fetch_columns.wait()
    for f in range(10):
        row = wrapped(start + row_distance(f), rows)
        slot = slots_ref[row]
        found = [jnp.int32(ZERO)] * SPAN
        found[BAND] = jnp.int32(f * TILES)
        offsets[f * TILES] = 0
        for v in range(1, TILES):
            offset = jnp.clip(signed(columns_ref[v, slot] - row, rows), -BAND, BAND)
            offsets[f * TILES + v] = offset
            for o in range(SPAN):
                if o != BAND:
                    found[o] = jnp.where(offset == o - BAND, f * TILES + v, found[o])
        for o in range(SPAN):
            tiles[row_place(f) * SPAN + o] = found[o]
    for side in (0, 1):
        for k in range(3, 6):
            place = 5 - k if side == 0 else 10 + k
            for o in range(SPAN):
                tiles[place * SPAN + o] = ZERO
            for n in range(WIDTHS[k]):
                offset = heading[side] * (BAND - WIDTHS[k] + 1 + n)
                tiles[place * SPAN + BAND + offset] = part_index(side, k) + n

    @pl.loop(0, 10)
    def _(f):
        stream = jnp.where(f < 7, heading[0], heading[1])
        k = jnp.where(f < 7, f - 4, f - 7)
        d = jnp.where(f < 4, f, jnp.where(stream > 0, -1 - k, count + k))
        for u in range(TILES):
            first = offsets[f * TILES + u]
            place = place_of(d + first)
            for t in range(TILES):
                offset = offsets[f * TILES + t] - first
                near = jnp.logical_and(offset <= BAND, offset >= -BAND)
                at = place * SPAN + BAND + jnp.where(near, offset, 0)
                names[f * NAMES + u * TILES + t] = jnp.where(near, tiles[at], ZERO)

    zeros = jnp.zeros((TILE, TILE), jnp.bfloat16)
    for pool in (e_high, e_low, f_high, f_low):
        pool[ZERO] = zeros
    for f in range(4):
        convert_whole(f)

    for k in range(1, 4):
        for side in (0, 1):
            await_row(side, k - 1)
            forward(side, k)
            convert_whole(4 + 3 * side + k - 1)

    def square(f):
        made = multiply(e_high, e_low, f * TILES, e_high, e_low, names, f * NAMES)
        for t in range(TILES):
            f_high[f * TILES + t], f_low[f * TILES + t] = split(made[t])

    pl.loop(0, 2)(square)
    for k in (4, 5):
        for side in (0, 1):
            await_row(side, k - 1)
            forward(side, k)
            convert_part(side, k - 1)
        if k == 4:
            pl.loop(2, 4)(square)
        pl.loop(0, 2)(lambda side: square(4 + 3 * side + (k - 4)))
    for side in (0, 1):
        await_row(side, 5)
        convert_part(side, 5)
    pl.loop(0, 2)(lambda side: square(4 + 3 * side + 2))

    @pl.loop(0, SLOT)
    def _(f):
        made = multiply(e_high, e_low, f * TILES, f_high, f_low, names, f * NAMES)
        scale = inverse_column(own_ref[f, 0], eye)
        for t in range(TILES):
            value = -(scale * own_ref[f, t])
            if t == 0:
                value = jnp.where(eye, 2.0, 0.0) + value
            at = f * TILES + t
            second = f_high[at].astype(jnp.float32) + f_low[at].astype(jnp.float32)
            value = value + (second + made[t])
            value = value * inverses[place_of(f + offsets[at])][0:1]
            out_ref[f, t] = jnp.where(f < count, value, 0.0)

    for side in (0, 1):
        for k in range(6):
            copy(side, k).wait_send()


def shards(coupling, columns, row_slots):
    devices = lax.axis_size(AXIS)
    windows = [pltpu.VMEM((w, TILE, TILE), jnp.float32) for w in WIDTHS] * 4
    pool = pltpu.VMEM((ZERO + 1, TILE, TILE), jnp.bfloat16)
    anywhere = pl.BlockSpec(memory_space=pl.ANY)
    by_tile = columns.T
    return pl.pallas_call(
        functools.partial(kernel, devices),
        out_shape=jax.ShapeDtypeStruct(coupling.shape, coupling.dtype),
        in_specs=[anywhere, anywhere, pl.BlockSpec(memory_space=pltpu.SMEM)],
        out_specs=pl.BlockSpec(memory_space=pltpu.VMEM),
        scratch_shapes=[
            pltpu.VMEM(coupling.shape, jnp.float32),
            pltpu.SMEM(by_tile.shape, jnp.int32),
        ]
        + windows
        + [pool] * 4
        + [
            pltpu.VMEM((PLACES, 8, TILE), jnp.float32),
            pltpu.SMEM((PLACES * SPAN,), jnp.int32),
            pltpu.SMEM((10 * TILES,), jnp.int32),
            pltpu.SMEM((10 * NAMES,), jnp.int32),
            pltpu.SemaphoreType.DMA((2, 6)),
            pltpu.SemaphoreType.DMA((2, 6)),
            pltpu.SemaphoreType.DMA,
            pltpu.SemaphoreType.DMA,
        ],
        compiler_params=pltpu.CompilerParams(collective_id=0, has_side_effects=True),
        name="iterate",
    )(coupling, by_tile, row_slots)


def solution(mesh):
    return jax.shard_map(
        shards,
        mesh=mesh,
        in_specs=(P(AXIS, None, None, None), P(), P()),
        out_specs=P(AXIS, None, None, None),
        check_vma=False,
    )
```

time: 286 us -> 47.8 us (0.17)
  starting transfers between devices: 102 us -> 0 us
  local copies, waits for them, and re-layouts: 68.1 us -> 2.5 us
  matrix products: 48.4 us -> 0 us
  Pallas kernels: 0 us -> 45.1 us
  other arithmetic: 33.7 us -> 0 us
  waiting for transfers between devices: 24.8 us -> 0 us
  between operations: 6.9 us -> 0.01 us
    ppermute x18 -> x0, starting transfers between devices: 102 us -> none  [from_behind(): return lax.ppermute(value, axis, pairs)]
    dot_general x16 -> x0, matrix products: 48.4 us -> none  [the longest x8 30.7 us: per_slot(): return jnp.einsum('kpq,kbqr->bpr', blocks, chosen, precision=precise)]
    pallas_call x0 -> x1, Pallas kernels: none -> 45.1 us  [shards(): pl.pallas_call(functools.partial(kernel, devices), out_shape=jax.ShapeDty...]
    gather x21 -> x0, local copies, waits for them, and re-layouts: 34.4 us -> none  [the longest x8 25.1 us: per_slot(): fetched = jnp.take(row_pool, located, axis=0)]
    ppermute x18 -> x0, waiting for transfers between devices: 24.8 us -> none  [from_behind(): return lax.ppermute(value, axis, pairs)]
    select_n x40 -> x0, other arithmetic: 18.3 us -> none  [the longest x10 12.4 us: held_rows(): return jnp.where(position < counts[device], starts[device] + position, -1)]
    unnamed x27 -> x1, local copies, waits for them, and re-layouts: 14.9 us -> 2.5 us
    dynamic_update_slice x16 -> x0, local copies, waits for them, and re-layouts: 7.33 us -> none  [pattern_product(): return lax.map(per_slot, (left, own_columns))]
  transfers between devices with their start and end apart: 18 -> 0, of which waited for: 5 -> 0; matrix products, arithmetic and copies ran while one was open for 12% -> 0% of each run, Pallas kernels for 0% -> 0%
where the time goes in v1:
time: 47.8 us; the launch traced here: 47.6 us
  Pallas kernels  45.1 us (94%)
  local copies, waits for them, and re-layouts  2.5 us (5%)
    pallas_call x1, Pallas kernels, shards(): pl.pallas_call(functools.partial(kernel, devices), out_shape=jax.ShapeDty...  45.1 us
    unnamed x1, local copies, waits for them, and re-layouts  2.5 us

profile of v1, /device:TPU:1, one launch (start us, length us, event | category | flops | bytes accessed | tf_op | source)
XLA Modules:
  0.0 47.6 jit_solution(15802197114659280223)
XLA Ops:
  0.0 45.1 %iterate.1 = f32[4,5,128,128]{3,2,1,0:T(8,128)} custom-call(f32[4,5,128,128]{3,2,1,0:T(8,128)} %own_hbm.1, s32[5,2048]{1,0:T(8,128)} %bitcast.1, s32[1024]{0:T(1024)} %slots_ref.1), custom_call_target="tpu_custom_call" | custom-call | tf_op jit(solution)/shard_map/iterate/pallas_call | solution.py:347
  45.1 2.5 %copy.5 = f32[4,5,128,128]{3,2,1,0:T(8,128)} copy(f32[4,5,128,128]{3,2,1,0:T(8,128)} %iterate.1) | data formatting | bytes 2621440

commit v2 on v1

--- a/solution.py
+++ b/solution.py
@@ -121,11 +121,13 @@
     return out
 
 
-def kernel(devices, own_hbm, columns_hbm, slots_ref, out_ref, own_ref, columns_ref, *refs):
+def kernel(
+    devices, own_hbm, columns_hbm, slots_hbm, out_ref, own_ref, columns_ref, slots_ref, *refs
+):
     arriving = (refs[0:6], refs[6:12])
     leaving = (refs[12:18], refs[18:24])
     e_high, e_low, f_high, f_low, inverses, tiles, offsets, names = refs[24:32]
-    send_sem, recv_sem, own_sem, columns_sem = refs[32:]
+    send_sem, recv_sem, own_sem, columns_sem, slots_sem = refs[32:]
     rows = slots_ref.shape[0]
     me = lax.axis_index(AXIS)
     right, left = lax.rem(me + 1, devices), lax.rem(me + devices - 1, devices)
@@ -137,11 +139,14 @@
     barrier = pltpu.get_barrier_semaphore()
     for other in (left, right):
         pl.semaphore_signal(barrier, inc=1, device_id=(other,), device_id_type=MESH)
+    fetch_slots = pltpu.make_async_copy(slots_hbm, slots_ref, slots_sem)
+    fetch_slots.start()
     fetch = pltpu.make_async_copy(own_hbm, own_ref, own_sem)
     fetch.start()
     fetch_columns = pltpu.make_async_copy(columns_hbm, columns_ref, columns_sem)
     fetch_columns.start()
 
+    fetch_slots.wait()
     start, count = ownership(slots_ref, me)
     shape = (TILE, TILE)
     eye = lax.broadcasted_iota(jnp.int32, shape, 0) == lax.broadcasted_iota(jnp.int32, shape, 1)
@@ -346,12 +351,13 @@
     by_tile = columns.T
     return pl.pallas_call(
         functools.partial(kernel, devices),
-        out_shape=jax.ShapeDtypeStruct(coupling.shape, coupling.dtype),
-        in_specs=[anywhere, anywhere, pl.BlockSpec(memory_space=pltpu.SMEM)],
+        out_shape=pltpu.VMEM(coupling.shape, coupling.dtype),
+        in_specs=[anywhere] * 3,
         out_specs=pl.BlockSpec(memory_space=pltpu.VMEM),
         scratch_shapes=[
             pltpu.VMEM(coupling.shape, jnp.float32),
             pltpu.SMEM(by_tile.shape, jnp.int32),
+            pltpu.SMEM(row_slots.shape, jnp.int32),
         ]
         + windows
         + [pool] * 4
@@ -364,6 +370,7 @@
             pltpu.SemaphoreType.DMA((2, 6)),
             pltpu.SemaphoreType.DMA,
             pltpu.SemaphoreType.DMA,
+            pltpu.SemaphoreType.DMA,
         ],
         compiler_params=pltpu.CompilerParams(collective_id=0, has_side_effects=True),
         name="iterate",

time: 47.8 us -> 44.5 us (0.931)
  Pallas kernels: 45.1 us -> 43.3 us
  local copies, waits for them, and re-layouts: 2.5 us -> 1.06 us
    pallas_call x1, Pallas kernels: 45.1 us -> 43.3 us  [shards(): pl.pallas_call(functools.partial(kernel, devices), out_shape=pltpu.VMEM(c...]
    unnamed x1, local copies, waits for them, and re-layouts: 2.5 us -> 1.06 us
where the time goes in v2:
time: 44.5 us; the launch traced here: 44.4 us
  Pallas kernels  43.3 us (97%)
  local copies, waits for them, and re-layouts  1.06 us (2%)
    pallas_call x1, Pallas kernels, shards(): pl.pallas_call(functools.partial(kernel, devices), out_shape=pltpu.VMEM(c...  43.3 us
    unnamed x1, local copies, waits for them, and re-layouts  1.06 us

profile of v2, /device:TPU:1, one launch (start us, length us, event | category | flops | bytes accessed | tf_op | source)
XLA Modules:
  0.0 44.4 jit_solution(1775557300350833401)
XLA Ops:
  0.0 43.3 %iterate.1 = f32[4,5,128,128]{3,2,1,0:T(8,128)S(1)} custom-call(f32[4,5,128,128]{3,2,1,0:T(8,128)} %own_hbm.1, s32[5,2048]{1,0:T(8,128)} %bitcast.1, s32[1024]{0:T(1024)} %slots_hbm.1), custom_call_target="tpu_custom_call" | custom-call | tf_op jit(solution)/shard_map/iterate/pallas_call | solution.py:352
  43.3 1.1 %copy.5 = f32[4,5,128,128]{3,2,1,0:T(8,128)} copy(f32[4,5,128,128]{3,2,1,0:T(8,128)S(1)} %iterate.1) | data formatting | bytes 2621440

commit v3 on v2

v3 whole, which is shorter than its diff:
```python
import functools

import jax
import jax.numpy as jnp
from jax import lax
from jax.experimental import pallas as pl
from jax.experimental.pallas import tpu as pltpu
from jax.sharding import PartitionSpec as P

TILE = 128
TILES = 5
SLOT = 4
BAND = 3
AXIS = "rows"
MESH = pl.DeviceIdType.MESH

WIDTHS = (5, 5, 5, 3, 2, 1)

WHOLE = 14 * TILES
PARTS = WIDTHS[3:]
ZERO = WHOLE + 2 * sum(PARTS)
SOURCES = 20
F_ROWS = 10
F_ZERO = F_ROWS * TILES
SPAN = 2 * BAND + 1
NAMES = TILES * TILES


def first_row(slots_ref, bound):
    found = jnp.int32(0)
    step = slots_ref.shape[0] // 2
    while step:
        below = slots_ref[found + step - 1] < bound
        found = found + jnp.where(below, step, 0)
        step //= 2
    return found


def held(slots_ref, start, device):
    rows = slots_ref.shape[0]
    count = jnp.int32(1)
    for k in range(1, SLOT):
        at = start + k
        inside = slots_ref[jnp.minimum(at, rows - 1)] < (device + 1) * SLOT
        count = count + jnp.where(jnp.logical_and(at < rows, inside), 1, 0)
    return count


def wrapped(value, rows):
    return lax.rem(value + rows, rows)


def signed(value, rows):
    half = rows // 2
    return lax.rem(value + rows + half, rows) - half


def inverse_column(tile, eye):
    return 1.0 / jnp.sum(jnp.where(eye, tile, 0.0), axis=1, keepdims=True)


def inverse_row(tile, eye):
    return 1.0 / jnp.sum(jnp.where(eye, tile, 0.0), axis=0, keepdims=True)


def split(value):
    high = value.astype(jnp.bfloat16)
    low = (value - high.astype(jnp.float32)).astype(jnp.bfloat16)
    return high, low


def dot(left, right):
    return jnp.dot(left, right, preferred_element_type=jnp.float32)


def multiply(left_high, left_low, base, pool_high, pool_low, names_ref, named):
    def block(pool, us, ts):
        return jnp.concatenate(
            [
                jnp.concatenate([pool[names_ref[named + u * TILES + t]] for t in ts], axis=1)
                for u in us
            ],
            axis=0,
        )

    def left(us):
        high = jnp.concatenate([left_high[base + u] for u in us], axis=1)
        low = jnp.concatenate([left_low[base + u] for u in us], axis=1)
        return high, jnp.concatenate([high, low], axis=0)

    pairs = ((0, 1), (2, 3))
    out = []
    for ts in pairs:
        total = None
        rest = None
        for us in pairs:
            high, both = left(us)
            part = dot(both, block(pool_high, us, ts))
            more = dot(high, block(pool_low, us, ts))
            total = part if total is None else total + part
            rest = more if rest is None else rest + more
        high = left_high[base + 4]
        low = left_low[base + 4]
        last = jnp.concatenate(
            [
                jnp.concatenate([high, high], axis=1),
                jnp.concatenate([low, jnp.zeros_like(low)], axis=1),
            ],
            axis=0,
        )
        right = jnp.concatenate([block(pool_high, (4,), ts), block(pool_low, (4,), ts)], axis=0)
        total = total + dot(last, right)
        value = total[:TILE] + total[TILE:] + rest
        out.append(value[:, :TILE])
        out.append(value[:, TILE:])
    total = None
    for us in pairs + ((4,),):
        right = jnp.concatenate([block(pool_high, us, (4,)), block(pool_low, us, (4,))], axis=1)
        part = dot(left(us)[1], right)
        total = part if total is None else total + part
    out.append(total[:TILE, :TILE] + (total[TILE:, :TILE] + total[:TILE, TILE:]))
    return out


def kernel(
    devices,
    own_hbm,
    columns_hbm,
    slots_hbm,
    out_ref,
    own_ref,
    partner_ref,
    columns_ref,
    slots_ref,
    *refs,
):
    leaving, arriving, passed = refs[0:6], refs[6:12], refs[12:18]
    e_high, e_low, f_high, f_low, inverses = refs[18:23]
    tiles, offsets, bases, names, f_names = refs[23:28]
    out_send, out_recv, pass_send, pass_recv, row_send, row_recv = refs[28:34]
    own_sem, columns_sem, slots_sem = refs[34:]
    rows = slots_ref.shape[0]
    me = lax.axis_index(AXIS)
    parity = lax.rem(me, 2)
    odd = parity == 1
    above, below = lax.rem(me + 2, devices), lax.rem(me + devices - 2, devices)
    outward = jnp.where(odd, above, below)
    partner = me + 1 - 2 * parity
    heading = 2 * parity - 1

    barrier = pltpu.get_barrier_semaphore()
    for other in (above, below, partner):
        pl.semaphore_signal(barrier, inc=1, device_id=(other,), device_id_type=MESH)
    fetch_slots = pltpu.make_async_copy(slots_hbm, slots_ref, slots_sem)
    fetch_slots.start()
    fetch = pltpu.make_async_copy(own_hbm, own_ref, own_sem)
    fetch.start()
    fetch_columns = pltpu.make_async_copy(columns_hbm, columns_ref, columns_sem)
    fetch_columns.start()

    shape = (TILE, TILE)
    eye = lax.broadcasted_iota(jnp.int32, shape, 0) == lax.broadcasted_iota(jnp.int32, shape, 1)

    fetch_slots.wait()
    chip_start = first_row(slots_ref, (me - parity) * SLOT)
    low_count = held(slots_ref, chip_start, me - parity)
    middle = chip_start + low_count
    high_count = held(slots_ref, middle, me - parity + 1)
    chip_end = middle + high_count
    start = jnp.where(odd, middle, chip_start)
    count = jnp.where(odd, high_count, low_count)
    partner_count = jnp.where(odd, low_count, high_count)
    partner_start = jnp.where(odd, chip_start, middle)

    fetch.wait()
    pl.semaphore_wait(barrier, 3)

    def remote(source, target, send, recv, device):
        return pltpu.make_async_remote_copy(
            src_ref=source,
            dst_ref=target,
            send_sem=send,
            recv_sem=recv,
            device_id=(device,),
            device_id_type=MESH,
        )

    def send_out(k):
        return remote(leaving[k], arriving[k], out_send.at[k], out_recv.at[k], outward)

    def pass_on(k):
        return remote(arriving[k], passed[k], pass_send.at[k], pass_recv.at[k], partner)

    share = remote(own_ref, partner_ref, row_send, row_recv, partner)

    def row_of(source):
        if source < 4:
            row = start + source
        elif source < 8:
            row = partner_start + (source - 4)
        elif source < 14:
            k = source - 8
            row = jnp.where(odd, chip_start - 1 - k, chip_end + k)
        else:
            k = source - 14
            row = jnp.where(odd, chip_end + k, chip_start - 1 - k)
        return wrapped(row, rows)

    def whole_row(source):
        return jnp.where(source < 11, source, source - 3)

    def source_of(m):
        inner = -1 - m
        beyond = 8 + inner - partner_count
        beside = 4 + jnp.where(odd, partner_count - 1 - inner, inner)
        own = jnp.where(odd, m, count - 1 - m)
        outer = 14 + m - count
        near = jnp.where(inner < partner_count, beside, beyond)
        source = jnp.where(m < 0, near, jnp.where(m < count, own, outer))
        return jnp.clip(source, 0, SOURCES - 1)

    def f_row_of(m):
        own = jnp.where(odd, m, count - 1 - m)
        row = jnp.where(m < 0, 3 - m, jnp.where(m < count, own, 7 + m - count))
        return jnp.clip(row, 0, F_ROWS - 1)

    def own_slot(k):
        return jnp.where(odd, jnp.maximum(count - 1 - k, 0), k)

    def partner_slot(inner):
        return jnp.clip(jnp.where(odd, partner_count - 1 - inner, inner), 0, SLOT - 1)

    def fill_whole(k):
        inner = k - count
        for t in range(TILES):
            value = own_ref[own_slot(k), t]
            if k > 0:
                value = jnp.where(inner >= 0, partner_ref[partner_slot(inner), t], value)
            for j in range(k - 1):
                value = jnp.where(inner - partner_count == j, arriving[j][t], value)
            leaving[k][t] = value

    def tile_at_offset(row, offset):
        slot = slots_ref[row]
        target = wrapped(row + offset, rows)
        found = jnp.int32(0)
        for v in range(1, TILES):
            found = jnp.where(columns_ref[v, slot] == target, v, found)
        return found

    def fill_part(k):
        inner = k - count
        beyond = inner - partner_count
        row = wrapped(jnp.where(odd, chip_end - 1 - k, chip_start + k), rows)

        def pick(t):
            value = partner_ref[partner_slot(inner), t]
            if k < SLOT:
                value = jnp.where(inner < 0, own_ref[own_slot(k), t], value)
            for j in range(min(k - 1, 3)):
                value = jnp.where(beyond == j, arriving[j][t], value)
            return value

        scale = inverse_column(pick(0), eye)
        for place in range(WIDTHS[k]):
            offset = heading * (BAND - WIDTHS[k] + 1 + place)
            index = tile_at_offset(row, offset)
            value = jnp.where(index > 0, -(scale * pick(index)), 0.0)
            for j in range(3, k - 1):
                ready = arriving[j][WIDTHS[j] - WIDTHS[k] + place]
                value = jnp.where(beyond == j, ready, value)
            leaving[k][place] = value

    def forward(k):
        if k < 3:
            fill_whole(k)
        else:
            fill_part(k)
        send_out(k).start()

    def convert_whole(e):
        if e < 4:
            source = own_ref.at[e]
        elif e < 8:
            source = partner_ref.at[e - 4]
        else:
            source = arriving[e - 8] if e < 11 else passed[e - 11]
        diagonal = source[0]
        scale = inverse_column(diagonal, eye)
        inverses[e] = jnp.broadcast_to(inverse_row(diagonal, eye), (8, TILE))
        for v in range(TILES):
            value = -(scale * source[v])
            if v == 0:
                value = jnp.where(eye, 1.0, 0.0) + value
            e_high[e * TILES + v], e_low[e * TILES + v] = split(value)

    def part_index(side, k):
        return WHOLE + side * sum(PARTS) + sum(PARTS[: k - 3])

    def convert_part(side, k):
        at = part_index(side, k)
        for n in range(WIDTHS[k]):
            e_high[at + n], e_low[at + n] = split((arriving, passed)[side][k][n])

    forward(0)
    share.start()

    fetch_columns.wait()
    for e in range(14):
        source = e if e < 11 else e + 3
        row = row_of(source)
        slot = slots_ref[row]
        found = [jnp.int32(ZERO)] * SPAN
        found[BAND] = jnp.int32(e * TILES)
        offsets[e * TILES] = 0
        for v in range(1, TILES):
            offset = jnp.clip(signed(columns_ref[v, slot] - row, rows), -BAND, BAND)
            offsets[e * TILES + v] = offset
            for o in range(SPAN):
                if o != BAND:
                    found[o] = jnp.where(offset == o - BAND, e * TILES + v, found[o])
        for o in range(SPAN):
            tiles[source * SPAN + o] = found[o]
    for side in (0, 1):
        for k in range(3, 6):
            source = 8 + 6 * side + k
            for o in range(SPAN):
                tiles[source * SPAN + o] = ZERO
            for n in range(WIDTHS[k]):
                offset = heading * (1 - 2 * side) * (BAND - WIDTHS[k] + 1 + n)
                tiles[source * SPAN + BAND + offset] = part_index(side, k) + n

    zeros = jnp.zeros((TILE, TILE), jnp.bfloat16)
    e_high[ZERO] = zeros
    e_low[ZERO] = zeros
    f_high[F_ZERO] = zeros
    f_low[F_ZERO] = zeros
    for e in range(4):
        convert_whole(e)

    share.wait_recv()
    forward(1)

    def distance(f):
        own = jnp.where(odd, f, count - 1 - f)
        return jnp.where(f < 4, own, jnp.where(f < 7, 3 - f, count + f - 7))

    @pl.loop(0, F_ROWS)
    def _(f):
        m = distance(f)
        source = jnp.where(f < 4, f, source_of(m))
        base = whole_row(source) * TILES
        bases[f] = base
        for u in range(TILES):
            first = offsets[base + u]
            at = source_of(m + heading * first)
            shift = f_row_of(m + heading * first) * TILES - whole_row(at) * TILES
            for t in range(TILES):
                offset = offsets[base + t] - first
                near = jnp.logical_and(offset <= BAND, offset >= -BAND)
                name = tiles[at * SPAN + BAND + jnp.where(near, offset, 0)]
                name = jnp.where(near, name, ZERO)
                names[f * NAMES + u * TILES + t] = name
                moved = jnp.clip(name + shift, 0, F_ZERO - 1)
                f_names[f * NAMES + u * TILES + t] = jnp.where(name == ZERO, F_ZERO, moved)

    for e in range(4, 8):
        convert_whole(e)

    def square(f):
        made = multiply(e_high, e_low, bases[f], e_high, e_low, names, f * NAMES)
        for t in range(TILES):
            f_high[f * TILES + t], f_low[f * TILES + t] = split(made[t])

    def receive(k):
        send_out(k).wait_recv()
        pass_on(k).start()

    def take(k):
        pass_on(k).wait_recv()
        if k < 3:
            convert_whole(11 + k)
        else:
            convert_part(1, k)

    for k in range(2, 6):
        receive(k - 2)
        forward(k)
        if k < 5:
            convert_whole(6 + k)
        else:
            convert_part(0, 3)
        if k > 2:
            take(k - 3)
    pl.loop(0, 4)(square)
    take(3)
    pl.loop(7, 8)(square)
    receive(4)
    convert_part(0, 4)
    pl.loop(4, 6)(square)
    take(4)
    pl.loop(8, 9)(square)
    receive(5)
    pl.loop(6, 7)(square)
    take(5)
    pl.loop(9, 10)(square)

    @pl.loop(0, SLOT)
    def _(f):
        made = multiply(e_high, e_low, f * TILES, f_high, f_low, f_names, f * NAMES)
        scale = inverse_column(own_ref[f, 0], eye)
        m = distance(f)
        for t in range(TILES):
            value = -(scale * own_ref[f, t])
            if t == 0:
                value = jnp.where(eye, 2.0, 0.0) + value
            at = f * TILES + t
            second = f_high[at].astype(jnp.float32) + f_low[at].astype(jnp.float32)
            value = value + (second + made[t])
            column = whole_row(source_of(m + heading * offsets[at]))
            value = value * inverses[jnp.minimum(column, 13)][0:1]
            out_ref[f, t] = jnp.where(f < count, value, 0.0)

    share.wait_send()
    for k in range(6):
        send_out(k).wait_send()
        pass_on(k).wait_send()


def shards(coupling, columns, row_slots):
    devices = lax.axis_size(AXIS)
    windows = [pltpu.VMEM((w, TILE, TILE), jnp.float32) for w in WIDTHS] * 3
    e_pool = pltpu.VMEM((ZERO + 1, TILE, TILE), jnp.bfloat16)
    f_pool = pltpu.VMEM((F_ZERO + 1, TILE, TILE), jnp.bfloat16)
    anywhere = pl.BlockSpec(memory_space=pl.ANY)
    by_tile = columns.T
    semaphore = pltpu.SemaphoreType.DMA
    return pl.pallas_call(
        functools.partial(kernel, devices),
        out_shape=pltpu.VMEM(coupling.shape, coupling.dtype),
        in_specs=[anywhere] * 3,
        out_specs=pl.BlockSpec(memory_space=pltpu.VMEM),
        scratch_shapes=[
            pltpu.VMEM(coupling.shape, jnp.float32),
            pltpu.VMEM(coupling.shape, jnp.float32),
            pltpu.SMEM(by_tile.shape, jnp.int32),
            pltpu.SMEM(row_slots.shape, jnp.int32),
        ]
        + windows
        + [e_pool, e_pool, f_pool, f_pool]
        + [
            pltpu.VMEM((14, 8, TILE), jnp.float32),
            pltpu.SMEM((SOURCES * SPAN,), jnp.int32),
            pltpu.SMEM((14 * TILES,), jnp.int32),
            pltpu.SMEM((F_ROWS,), jnp.int32),
            pltpu.SMEM((F_ROWS * NAMES,), jnp.int32),
            pltpu.SMEM((F_ROWS * NAMES,), jnp.int32),
        ]
        + [semaphore((6,))] * 4
        + [semaphore] * 5,
        compiler_params=pltpu.CompilerParams(collective_id=0, has_side_effects=True),
        name="iterate",
    )(coupling, by_tile, row_slots)


def solution(mesh):
    return jax.shard_map(
        shards,
        mesh=mesh,
        in_specs=(P(AXIS, None, None, None), P(), P()),
        out_specs=P(AXIS, None, None, None),
        check_vma=False,
    )
```

time: 44.5 us -> 40.4 us (0.908)
  Pallas kernels: 43.3 us -> 39.2 us
    pallas_call x1, Pallas kernels: 43.3 us -> 39.2 us  [shards(): pl.pallas_call(functools.partial(kernel, devices), out_shape=pltpu.VMEM(c...]
where the time goes in v3:
time: 40.4 us; the launch traced here: 40.2 us
  Pallas kernels  39.2 us (97%)
  local copies, waits for them, and re-layouts  1.06 us (3%)
    pallas_call x1, Pallas kernels, shards(): pl.pallas_call(functools.partial(kernel, devices), out_shape=pltpu.VMEM(c...  39.2 us
    unnamed x1, local copies, waits for them, and re-layouts  1.06 us

profile of v3, /device:TPU:1, one launch (start us, length us, event | category | flops | bytes accessed | tf_op | source)
XLA Modules:
  0.0 40.2 jit_solution(11390186749960464143)
XLA Ops:
  0.0 39.2 %iterate.1 = f32[4,5,128,128]{3,2,1,0:T(8,128)S(1)} custom-call(f32[4,5,128,128]{3,2,1,0:T(8,128)} %own_hbm.1, s32[5,2048]{1,0:T(8,128)} %bitcast.1, s32[1024]{0:T(1024)} %slots_hbm.1), custom_call_target="tpu_custom_call" | custom-call | tf_op jit(solution)/shard_map/iterate/pallas_call | solution.py:438
  39.2 1.1 %copy.5 = f32[4,5,128,128]{3,2,1,0:T(8,128)} copy(f32[4,5,128,128]{3,2,1,0:T(8,128)S(1)} %iterate.1) | data formatting | bytes 2621440

commit v4 on v3

--- a/solution.py
+++ b/solution.py
@@ -12,6 +12,7 @@
 SLOT = 4
 BAND = 3
 AXIS = "rows"
+RUN = 128
 MESH = pl.DeviceIdType.MESH
 
 WIDTHS = (5, 5, 5, 3, 2, 1)
@@ -172,8 +173,6 @@
     partner_count = jnp.where(odd, low_count, high_count)
     partner_start = jnp.where(odd, chip_start, middle)
 
-    fetch.wait()
-    pl.semaphore_wait(barrier, 3)
 
     def remote(source, target, send, recv, device):
         return pltpu.make_async_remote_copy(
@@ -302,7 +301,10 @@
         for n in range(WIDTHS[k]):
             e_high[at + n], e_low[at + n] = split((arriving, passed)[side][k][n])
 
-    forward(0)
+    fetch.wait()
+    fill_whole(0)
+    pl.semaphore_wait(barrier, 3)
+    send_out(0).start()
     share.start()
 
     fetch_columns.wait()
@@ -383,6 +385,22 @@
         else:
             convert_part(1, k)
 
+    place = lax.rem(me, RUN)
+    late_up = place == 1
+    late_passed = place == 0
+
+    def squares(first, last):
+        pl.loop(first, last)(square)
+
+    def choose(up, other):
+        return jnp.where(late_up, up, other)
+
+    @pl.when(late_up)
+    def _():
+        for k in range(6):
+            take(k)
+
+    squares(8, choose(10, 8))
     for k in range(2, 6):
         receive(k - 2)
         forward(k)
@@ -391,19 +409,53 @@
         else:
             convert_part(0, 3)
         if k > 2:
-            take(k - 3)
-    pl.loop(0, 4)(square)
-    take(3)
-    pl.loop(7, 8)(square)
-    receive(4)
-    convert_part(0, 4)
-    pl.loop(4, 6)(square)
-    take(4)
-    pl.loop(8, 9)(square)
-    receive(5)
-    pl.loop(6, 7)(square)
-    take(5)
-    pl.loop(9, 10)(square)
+
+            @pl.when(place > 1)
+            def _():
+                take(k - 3)
+
+        if k == 4:
+            squares(0, choose(5, 0))
+
+    @pl.when(late_passed)
+    def _():
+        receive(4)
+        convert_part(0, 4)
+        receive(5)
+
+    squares(6, jnp.where(late_passed, 7, 6))
+
+    @pl.when(late_passed)
+    def _():
+        for k in range(3):
+            take(k)
+
+    squares(choose(5, 0), choose(6, 4))
+
+    def take_unless_taken(k):
+        @pl.when(jnp.logical_not(late_up))
+        def _():
+            take(k)
+
+    take_unless_taken(3)
+    squares(7, 8)
+
+    @pl.when(jnp.logical_not(late_passed))
+    def _():
+        receive(4)
+        convert_part(0, 4)
+
+    squares(choose(6, 4), 6)
+    take_unless_taken(4)
+    squares(choose(9, 8), 9)
+    squares(jnp.where(late_passed, 7, 6), 7)
+
+    @pl.when(jnp.logical_not(late_passed))
+    def _():
+        receive(5)
+
+    take_unless_taken(5)
+    squares(choose(10, 9), 10)
 
     @pl.loop(0, SLOT)
     def _(f):

time: 40.4 us -> 47.7 us (1.18)
  the two profiles are of different devices: /device:TPU:1 before, /device:TPU:3 now
where the time goes in v4:
time: 47.7 us; the launch traced here: 47.6 us
  Pallas kernels  46.5 us (97%)
  local copies, waits for them, and re-layouts  1.06 us (2%)
    pallas_call x1, Pallas kernels, shards(): pl.pallas_call(functools.partial(kernel, devices), out_shape=pltpu.VMEM(c...  46.5 us
    unnamed x1, local copies, waits for them, and re-layouts  1.06 us

profile of v4, /device:TPU:3, one launch (start us, length us, event | category | flops | bytes accessed | tf_op | source)
XLA Modules:
  0.0 47.6 jit_solution(17424588638619903111)
XLA Ops:
  0.0 46.5 %iterate.1 = f32[4,5,128,128]{3,2,1,0:T(8,128)S(1)} custom-call(f32[4,5,128,128]{3,2,1,0:T(8,128)} %own_hbm.1, s32[5,2048]{1,0:T(8,128)} %bitcast.1, s32[1024]{0:T(1024)} %slots_hbm.1), custom_call_target="tpu_custom_call" | custom-call | tf_op jit(solution)/shard_map/iterate/pallas_call | solution.py:490
  46.5 1.1 %copy.5 = f32[4,5,128,128]{3,2,1,0:T(8,128)} copy(f32[4,5,128,128]{3,2,1,0:T(8,128)S(1)} %iterate.1) | data formatting | bytes 2621440

commit v5 on v3

--- a/solution.py
+++ b/solution.py
@@ -12,6 +12,7 @@
 SLOT = 4
 BAND = 3
 AXIS = "rows"
+RUN = 128
 MESH = pl.DeviceIdType.MESH
 
 WIDTHS = (5, 5, 5, 3, 2, 1)
@@ -172,8 +173,6 @@
     partner_count = jnp.where(odd, low_count, high_count)
     partner_start = jnp.where(odd, chip_start, middle)
 
-    fetch.wait()
-    pl.semaphore_wait(barrier, 3)
 
     def remote(source, target, send, recv, device):
         return pltpu.make_async_remote_copy(
@@ -302,7 +301,10 @@
         for n in range(WIDTHS[k]):
             e_high[at + n], e_low[at + n] = split((arriving, passed)[side][k][n])
 
-    forward(0)
+    fetch.wait()
+    fill_whole(0)
+    pl.semaphore_wait(barrier, 3)
+    send_out(0).start()
     share.start()
 
     fetch_columns.wait()
@@ -383,30 +385,23 @@
         else:
             convert_part(1, k)
 
-    for k in range(2, 6):
-        receive(k - 2)
-        forward(k)
-        if k < 5:
-            convert_whole(6 + k)
-        else:
-            convert_part(0, 3)
-        if k > 2:
-            take(k - 3)
-    pl.loop(0, 4)(square)
-    take(3)
-    pl.loop(7, 8)(square)
-    receive(4)
-    convert_part(0, 4)
-    pl.loop(4, 6)(square)
-    take(4)
-    pl.loop(8, 9)(square)
-    receive(5)
-    pl.loop(6, 7)(square)
-    take(5)
-    pl.loop(9, 10)(square)
-
-    @pl.loop(0, SLOT)
-    def _(f):
+    place = lax.rem(me, RUN)
+    late = place < 4
+    late_odd = jnp.logical_and(late, odd)
+    late_even = jnp.logical_and(late, jnp.logical_not(odd))
+    prompt = jnp.logical_not(late)
+    not_late_even = jnp.logical_not(late_even)
+
+    def squares(first, last):
+        pl.loop(first, last)(square)
+
+    def take_rows(condition, ks):
+        @pl.when(condition)
+        def _():
+            for k in ks:
+                take(k)
+
+    def finish(f):
         made = multiply(e_high, e_low, f * TILES, f_high, f_low, f_names, f * NAMES)
         scale = inverse_column(own_ref[f, 0], eye)
         m = distance(f)
@@ -420,6 +415,53 @@
             column = whole_row(source_of(m + heading * offsets[at]))
             value = value * inverses[jnp.minimum(column, 13)][0:1]
             out_ref[f, t] = jnp.where(f < count, value, 0.0)
+
+    for k in range(2, 6):
+        receive(k - 2)
+        forward(k)
+        if k < 5:
+            convert_whole(6 + k)
+        else:
+            convert_part(0, 3)
+        if k == 3:
+            take_rows(late_odd, (0, 1, 2))
+        if k > 2:
+            take_rows(prompt, (k - 3,))
+        if k == 4:
+            squares(jnp.where(late_odd, 0, 4), jnp.where(late_even, 4, 5))
+
+    @pl.when(late_even)
+    def _():
+        receive(4)
+        convert_part(0, 4)
+        receive(5)
+
+    squares(6, jnp.where(late_even, 7, 6))
+    take_rows(late_even, (0, 1))
+    squares(jnp.where(late_even, 4, 5), 6)
+    take_rows(late_even, (2,))
+    squares(jnp.where(late_odd, 4, 0), 4)
+    take(3)
+    squares(7, 8)
+    pl.loop(2, jnp.where(late_even, 4, 2))(finish)
+
+    @pl.when(not_late_even)
+    def _():
+        receive(4)
+        convert_part(0, 4)
+
+    squares(jnp.where(late_even, 7, 6), 7)
+    take(4)
+    squares(8, 9)
+    pl.loop(1, jnp.where(late_even, 2, 1))(finish)
+
+    @pl.when(not_late_even)
+    def _():
+        receive(5)
+
+    take(5)
+    squares(9, 10)
+    pl.loop(0, jnp.where(late_even, 1, 4))(finish)
 
     share.wait_send()
     for k in range(6):

time: 40.4 us -> 39.9 us (0.988)
  Pallas kernels: 39.2 us -> 38.7 us
    pallas_call x1, Pallas kernels: 39.2 us -> 38.7 us  [shards(): pl.pallas_call(functools.partial(kernel, devices), out_shape=pltpu.VMEM(c...]
where the time goes in v5:
time: 39.9 us; the launch traced here: 39.8 us
  Pallas kernels  38.7 us (97%)
  local copies, waits for them, and re-layouts  1.06 us (3%)
    pallas_call x1, Pallas kernels, shards(): pl.pallas_call(functools.partial(kernel, devices), out_shape=pltpu.VMEM(c...  38.7 us
    unnamed x1, local copies, waits for them, and re-layouts  1.06 us

profile of v5, /device:TPU:1, one launch (start us, length us, event | category | flops | bytes accessed | tf_op | source)
XLA Modules:
  0.0 39.8 jit_solution(15782153150583780549)
XLA Ops:
  0.0 38.7 %iterate.1 = f32[4,5,128,128]{3,2,1,0:T(8,128)S(1)} custom-call(f32[4,5,128,128]{3,2,1,0:T(8,128)} %own_hbm.1, s32[5,2048]{1,0:T(8,128)} %bitcast.1, s32[1024]{0:T(1024)} %slots_hbm.1), custom_call_target="tpu_custom_call" | custom-call | tf_op jit(solution)/shard_map/iterate/pallas_call | solution.py:480
  38.7 1.1 %copy.5 = f32[4,5,128,128]{3,2,1,0:T(8,128)} copy(f32[4,5,128,128]{3,2,1,0:T(8,128)S(1)} %iterate.1) | data formatting | bytes 2621440
